TPU v7x, 32 devices: a whole 2x2x4 slice. The times are simulated.
32 devices in a mesh: lon: 8 (over z, x), lat: 4 (over y, core).
Axes of the slice: x: 2, y: 2, z: 4, core: 2. Of those that a mesh axis runs over, the one named last changes fastest.
Arguments:
- state: float32 [2048, 64, 1024], P('lon', None, 'lat'), may hold values from -6 to 6
Outputs:
- spectrum: float32 [2, 1024, 64, 1024], P(None, 'lon', None, 'lat')
All inputs are finite; a program needn't handle non-finite values.
Results may differ from a plain program's by a relative error of at most 0.00011.
Values sent between devices are 32-bit elements; how exact they have to be, the bound alone decides.
A program may use at most 128 MiB of HBM per device.

v0:
```python
import math

import jax
import jax.numpy as jnp
from jax import lax
from jax.sharding import PartitionSpec as P


def phase_angle(first_index, second_index, period):
    product = first_index * second_index % period
    return product.astype(jnp.float32) * (2.0 * math.pi / period)


def dense_spectrum(gathered, factor):
    lon_count = gathered.shape[0]
    mode_count = lon_count // 2
    wavenum = lax.broadcasted_iota(jnp.int32, (mode_count, lon_count), 0)
    longitude = lax.broadcasted_iota(jnp.int32, (mode_count, lon_count), 1)
    angles = phase_angle(wavenum, longitude, lon_count)
    real_part = jnp.dot(
        jnp.cos(angles) * factor,
        gathered,
        precision=lax.Precision.HIGHEST,
        preferred_element_type=jnp.float32,
    )
    imag_part = jnp.dot(
        -jnp.sin(angles) * factor,
        gathered,
        precision=lax.Precision.HIGHEST,
        preferred_element_type=jnp.float32,
    )
    return jnp.stack([real_part, imag_part])


def local(state):
    lon_dev, fields, lat_dev = state.shape
    devices = lax.axis_size("lon")
    columns = state.reshape(lon_dev, fields * lat_dev)
    factor = 1.0 / math.sqrt(lon_dev * devices)
    gathered = lax.all_to_all(columns, "lon", split_axis=1, concat_axis=0, tiled=True)
    spectrum = dense_spectrum(gathered, factor)
    shares = lax.all_to_all(spectrum, "lon", split_axis=1, concat_axis=2, tiled=True)
    return shares.reshape(2, shares.shape[1], fields, lat_dev)


def solution(mesh):
    return jax.shard_map(
        local,
        mesh=mesh,
        in_specs=(P("lon", None, "lat"),),
        out_specs=P(None, "lon", None, "lat"),
        check_vma=False,
    )
```

profile of v0, /device:TPU:13, one launch (start us, length us, event | category | flops | bytes accessed | tf_op | source)
XLA Modules:
  0.0 962.6 jit_solution(15890371982656909931)
XLA Ops:
  0.0 17.6 %copy.7 = f32[256,64,256]{0,2,1:T(8,128)} copy(f32[256,64,256]{2,1,0:T(8,128)} %param.1) | data formatting | bytes 33554432 | tf_op args[0]
  17.6 5.8 all-to-all-start
  23.4 31.5 %fusion.41 = f32[1024,2048]{1,0:T(8,128)} fusion(), kind=kLoop, calls=%fused_computation.12.clone.clone.clone.1 | loop fusion | flops 31457280 | bytes 8388608 | tf_op jit(solution)/shard_map/dot_general | solution.py:20
  54.9 31.9 %fusion.43 = f32[1024,2048]{1,0:T(8,128)} fusion(), kind=kLoop, calls=%fused_computation.8.clone.clone.clone.1 | loop fusion | flops 33554432 | bytes 8388608 | tf_op jit(solution)/shard_map/dot_general | solution.py:26
  86.8 297.8 %all-to-all-done = f32[256,8,2048]{0,2,1:T(8,128)} async-done(((f32[256,8,2048]{0,2,1:T(8,128)}), f32[256,8,2048]{0,2,1:T(8,128)}, u32[]{:S(2)}, u32[]{:S(2)}) %all-to-all-start) | async-done | bytes 16777248 | tf_op jit(solution)/shard_map/all_to_all | solution.py:40
  384.6 16.3 %copy.8 = f32[8,256,2048]{2,1,0:T(8,128)} copy(f32[8,256,2048]{1,2,0:T(8,128)} %bitcast.1) | data formatting | bytes 33554432 | tf_op jit(solution)/shard_map/all_to_all | solution.py:40
  400.9 0.0 copy-start
  400.9 68.6 %fusion.13 = f32[1,1024,2048]{2,1,0:T(8,128)} fusion(f32[2048,2048]{1,0:T(8,128)} %bitcast.22, f32[1024,2048]{1,0:T(8,128)} %fusion.41), kind=kOutput, calls=%fused_computation.17 | convolution fusion | flops 51539607552 | bytes 33554432 | tf_op jit(solution)/shard_map/dot_general | solution.py:20
  469.5 0.0 copy-done
  469.5 61.1 %fusion.16 = f32[1,1024,2048]{2,1,0:T(8,128)} fusion(f32[2048,2048]{1,0:T(8,128)S(1)} %bitcast.23, f32[1024,2048]{1,0:T(8,128)} %fusion.43), kind=kOutput, calls=%fused_computation.18 | convolution fusion | flops 51539607552 | bytes 33554432 | tf_op jit(solution)/shard_map/dot_general | solution.py:26
  530.6 6.5 pad_maximum_fusion
  537.1 21.3 %copy.9 = f32[2,1024,2048]{2,0,1:T(2,128)} copy(f32[2,1024,2048]{2,1,0:T(8,128)S(1)} %pad_maximum_fusion) | data formatting | bytes 33554432 | tf_op jit(solution)/shard_map/stack | solution.py:32
  558.5 366.4 %all_to_all.34 = f32[2,1024,2048]{2,0,1:T(2,128)S(1)} all-to-all(f32[2,1024,2048]{2,0,1:T(2,128)} %copy.9), channel_id=1, replica_groups=mesh['lon'=8,'lat'=4] {'lon'}, dimensions={1} | all-to-all | bytes 33554432 | tf_op jit(solution)/shard_map/all_to_all | solution.py:42
  924.9 19.8 %copy.10 = f32[2,128,8,2048]{3,2,1,0:T(8,128)} copy(f32[2,128,8,2048]{3,0,1,2:T(2,128)S(1)} %bitcast.21) | data formatting | bytes 33554432 | tf_op jit(solution)/shard_map/all_to_all | solution.py:42
  944.7 18.0 %reshape.9 = f32[2,128,64,256]{3,2,1,0:T(8,128)} reshape(f32[2,128,8,2048]{3,2,1,0:T(8,128)} %copy.10) | data formatting | bytes 33554432 | tf_op jit(solution)/shard_map/reshape | solution.py:43
Async XLA Ops:
  17.6 367.0 %all-to-all-start = ((f32[256,8,2048]{0,2,1:T(8,128)}), f32[256,8,2048]{0,2,1:T(8,128)}, u32[]{:S(2)}, u32[]{:S(2)}) async-start(f32[256,8,2048]{0,2,1:T(8,128)} %bitcast.20), calls=%async_computation | async-start | bytes 33554432 | tf_op jit(solution)/shard_map/all_to_all | solution.py:40
  400.9 68.6 %copy-start = (f32[8,256,2048]{2,1,0:T(8,128)S(1)}, f32[8,256,2048]{2,1,0:T(8,128)}, u32[]{:S(2)}) copy-start(f32[8,256,2048]{2,1,0:T(8,128)} %copy.8) | copy-start | bytes 50331652
where the time goes:
time: 968 us; the launch traced here: 963 us
  blocking collectives  366 us (38%)
  waiting for transfers between devices  298 us (31%)
  matrix products  130 us (13%)
  local copies, waits for them, and re-layouts  93 us (10%)
  other arithmetic  69.9 us (7%)
    all_to_all x1, blocking collectives, local(): lax.all_to_all(spectrum, 'lon', split_axis=1, concat_axis=2, tiled=True)  366 us
    all_to_all x1, waiting for transfers between devices, local(): lax.all_to_all(columns, 'lon', split_axis=1, concat_axis=0, tiled=True)  298 us
    dot_general x1, matrix products, dense_spectrum(): jnp.dot(jnp.cos(angles) * factor, gathered, precision=lax.Precision.HIGHE...  68.6 us
    dot_general x1, matrix products, dense_spectrum(): jnp.dot(-jnp.sin(angles) * factor, gathered, precision=lax.Precision.HIGH...  61.1 us
    dot_general x1, other arithmetic, dense_spectrum(): jnp.dot(-jnp.sin(angles) * factor, gathered, precision=lax.Precision.HIGH...  31.9 us
    dot_general x1, other arithmetic, dense_spectrum(): jnp.dot(jnp.cos(angles) * factor, gathered, precision=lax.Precision.HIGHE...  31.5 us
    another operation x1, local copies, waits for them, and re-layouts, dense_spectrum(): return jnp.stack([real_part, imag_part])  21.3 us
    all_to_all x1, local copies, waits for them, and re-layouts, local(): lax.all_to_all(spectrum, 'lon', split_axis=1, concat_axis=2, tiled=True)  19.8 us
  transfers between devices with their start and end apart: 1, of which 1 were waited for; matrix products, arithmetic and copies ran while one was open for 7% of the time, Pallas kernels for 0%

commit v1 on v0

--- a/solution.py
+++ b/solution.py
@@ -1,9 +1,18 @@
+import functools
 import math
 
 import jax
 import jax.numpy as jnp
+import numpy as np
 from jax import lax
+from jax.experimental import pallas as pl
+from jax.experimental.pallas import tpu as pltpu
 from jax.sharding import PartitionSpec as P
+
+RADIX = 8
+LANES = 128
+SUBLANES = 8
+TILE = 16
 
 
 def phase_angle(first_index, second_index, period):
@@ -32,7 +41,7 @@
     return jnp.stack([real_part, imag_part])
 
 
-def local(state):
+def dense_local(state):
     lon_dev, fields, lat_dev = state.shape
     devices = lax.axis_size("lon")
     columns = state.reshape(lon_dev, fields * lat_dev)
@@ -43,7 +52,256 @@
     return shares.reshape(2, shares.shape[1], fields, lat_dev)
 
 
+def split(value):
+    high = value.astype(jnp.bfloat16)
+    return high, (value - high.astype(jnp.float32)).astype(jnp.bfloat16)
+
+
+def build_weights(cos_base, sin_base, cos_turn, sin_turn, w_hi, w_lo):
+    modes, points = cos_base.shape
+
+    def put(group, row, column, value):
+        high, low = split(value)
+        rows, columns = pl.ds(row * modes, modes), pl.ds(column * points, points)
+        w_hi[group, rows, columns] = high
+        w_lo[group, rows, columns] = low
+
+    def table(residue):
+        turn_c = cos_turn[pl.ds(residue, 1), :]
+        turn_s = sin_turn[pl.ds(residue, 1), :]
+        cos_b, sin_b = cos_base[...], sin_base[...]
+        return cos_b * turn_c - sin_b * turn_s, sin_b * turn_c + cos_b * turn_s
+
+    zero = jnp.zeros((modes, points), jnp.float32)
+    for group in range(RADIX // 2):
+        cos_a, sin_a = table(group)
+        if group == 0:
+            cos_b, sin_b = table(RADIX // 2)
+            entries = ((cos_a, zero), (-sin_a, zero), (zero, cos_b), (zero, -sin_b))
+        else:
+            cos_b, sin_b = table(RADIX - group)
+            entries = ((cos_a, sin_a), (-sin_a, cos_a), (cos_b, -sin_b), (-sin_b, -cos_b))
+        for row, pair in enumerate(entries):
+            for column, value in enumerate(pair):
+                put(group, row, column, value)
+
+
+def radix_stage(x):
+    root = math.sqrt(0.5)
+    a, b, c, d = x[0] + x[4], x[0] - x[4], x[2] + x[6], x[2] - x[6]
+    e, f, g, h = x[1] + x[5], x[1] - x[5], x[3] + x[7], x[3] - x[7]
+    even, odd = a + c, e + g
+    diff, total = root * (f - h), root * (f + h)
+    return (
+        (even + odd, even - odd),
+        (b + diff, -d - total),
+        (a - c, g - e),
+        (b - diff, d - total),
+    )
+
+
+def transform(half, points, grid, packed, w_hi, w_lo, y_hi, y_lo):
+    modes = points // 2
+    share = modes // RADIX
+    block_rows = share * RADIX
+    grid_rows = grid.reshape(grid.shape[0] * RADIX * points * SUBLANES, LANES)
+    packed_rows = packed.reshape(packed.shape[0] * RADIX * 2 * block_rows * SUBLANES, LANES)
+
+    def field_pair(pair, carry):
+        def tile(index, carry):
+            first = index * TILE
+            for side in range(2):
+                x = [
+                    grid_rows[
+                        pl.ds(
+                            ((half * RADIX + d) * points + first) * SUBLANES + 2 * pair + side,
+                            TILE,
+                            stride=SUBLANES,
+                        ),
+                        :,
+                    ]
+                    for d in range(RADIX)
+                ]
+                for group, values in enumerate(radix_stage(x)):
+                    for part, value in enumerate(values):
+                        high, low = split(value)
+                        rows = pl.ds(pl.multiple_of(part * points + first, TILE), TILE)
+                        lanes = pl.ds(side * LANES, LANES)
+                        y_hi[group, rows, lanes] = high
+                        y_lo[group, rows, lanes] = low
+            return carry
+
+        lax.fori_loop(0, points // TILE, tile, 0)
+
+        def residues(group, carry):
+            dot = functools.partial(jnp.dot, preferred_element_type=jnp.float32)
+            high = y_hi[group]
+            out = dot(w_hi[group], high) + dot(w_hi[group], y_lo[group]) + dot(w_lo[group], high)
+            other = jnp.where(group == 0, RADIX // 2, RADIX - group)
+            for which, residue in enumerate((group, other)):
+                for part in range(2):
+                    row = (2 * which + part) * modes
+                    for e in range(RADIX):
+                        for side in range(2):
+                            base = ((half * RADIX + e) * 2 + part) * block_rows
+                            packed_rows[
+                                pl.ds(
+                                    (base + residue) * SUBLANES + 2 * pair + side,
+                                    share,
+                                    stride=RADIX * SUBLANES,
+                                ),
+                                :,
+                            ] = out[
+                                row + e * share : row + (e + 1) * share,
+                                side * LANES : (side + 1) * LANES,
+                            ]
+            return carry
+
+        lax.fori_loop(0, RADIX // 2, residues, 0)
+        return carry
+
+    lax.fori_loop(0, SUBLANES // 2, field_pair, 0)
+
+
+def kernel(
+    halves,
+    state, cos_base, sin_base, cos_turn, sin_turn, out,
+    grid, packed, w_hi, w_lo, y_hi, y_lo,
+    send_sem, recv_sem, own_sem,
+):
+    points = state.shape[0]
+    me = lax.axis_index("lon")
+    ring, side = me // 2, lax.rem(me, 2)
+
+    def peer(dz, dx):
+        return lax.rem(ring + dz + 4, 4) * 2 + lax.rem(side + dx, 2)
+
+    offsets = [(2, 1), (2, 0), (1, 1), (1, 0), (3, 1), (3, 0), (0, 1)]
+
+    def fields(owner):
+        return pl.ds(pl.multiple_of(owner * SUBLANES, SUBLANES), SUBLANES)
+
+    def lanes(half):
+        return pl.ds(half * LANES, LANES)
+
+    def source(phase, half, target):
+        if phase == 0:
+            return state.at[:, fields(target), lanes(half)]
+        return packed.at[half, target]
+
+    def landing(phase, half, origin):
+        if phase == 0:
+            return grid.at[half, origin]
+        return out.at[:, :, fields(origin), lanes(half)]
+
+    def direct(phase, half, index):
+        target = peer(*offsets[index])
+        return pltpu.make_async_remote_copy(
+            src_ref=source(phase, half, target),
+            dst_ref=landing(phase, half, me),
+            send_sem=send_sem.at[phase, half, index],
+            recv_sem=recv_sem.at[phase, half, index],
+            device_id={"lon": target},
+            device_id_type=pl.DeviceIdType.MESH,
+        )
+
+    def own(phase, half):
+        return pltpu.make_async_copy(
+            source(phase, half, me), landing(phase, half, me), own_sem.at[phase, half]
+        )
+
+    def send(phase, half):
+        for index in range(len(offsets)):
+            direct(phase, half, index).start()
+        own(phase, half).start()
+
+    def receive(phase, half):
+        own(phase, half).wait()
+        for index, (dz, dx) in enumerate(offsets):
+            origin = peer(-dz, dx)
+            pltpu.make_async_remote_copy(
+                src_ref=landing(phase, half, origin),
+                dst_ref=landing(phase, half, origin),
+                send_sem=send_sem.at[phase, half, index],
+                recv_sem=recv_sem.at[phase, half, index],
+                device_id={"lon": origin},
+                device_id_type=pl.DeviceIdType.MESH,
+            ).wait_recv()
+
+    barrier = pltpu.get_barrier_semaphore()
+    for dz, dx in offsets:
+        pl.semaphore_signal(
+            barrier, inc=1, device_id={"lon": peer(dz, dx)}, device_id_type=pl.DeviceIdType.MESH
+        )
+    pl.semaphore_wait(barrier, len(offsets))
+
+    for half in range(halves):
+        send(0, half)
+    build_weights(cos_base, sin_base, cos_turn, sin_turn, w_hi, w_lo)
+    for half in range(halves):
+        receive(0, half)
+        transform(half, points, grid, packed, w_hi, w_lo, y_hi, y_lo)
+        send(1, half)
+    for half in range(halves):
+        receive(1, half)
+    for phase in range(2):
+        for half in range(halves):
+            for index in range(len(offsets)):
+                direct(phase, half, index).wait_send()
+
+
+def angle_tables(points):
+    count = points * RADIX
+    scale = 1.0 / math.sqrt(count)
+    place = np.arange(points)
+    base = 2.0 * np.pi / count * (RADIX * np.arange(points // 2)[:, None] * place % count)
+    turn = 2.0 * np.pi / count * (np.arange(RADIX)[:, None] * place % count)
+    tables = (scale * np.cos(base), scale * np.sin(base), np.cos(turn), np.sin(turn))
+    return [jnp.asarray(table.astype(np.float32)) for table in tables]
+
+
+def fused_local(state):
+    points, fields, lat_dev = state.shape
+    halves = lat_dev // LANES
+    modes = points // 2
+    vmem = pl.BlockSpec(memory_space=pltpu.VMEM)
+    hbm = pl.BlockSpec(memory_space=pl.ANY)
+    half_shape = (2, modes, SUBLANES, LANES)
+    return pl.pallas_call(
+        functools.partial(kernel, halves),
+        out_shape=jax.ShapeDtypeStruct((2, modes, fields, lat_dev), jnp.float32),
+        in_specs=[hbm] + [vmem] * 4,
+        out_specs=hbm,
+        scratch_shapes=[
+            pltpu.VMEM((halves, RADIX, points, SUBLANES, LANES), jnp.float32),
+            pltpu.VMEM((halves, RADIX) + half_shape, jnp.float32),
+            pltpu.VMEM((RADIX // 2, 4 * modes, 2 * points), jnp.bfloat16),
+            pltpu.VMEM((RADIX // 2, 4 * modes, 2 * points), jnp.bfloat16),
+            pltpu.VMEM((RADIX // 2, 2 * points, 2 * LANES), jnp.bfloat16),
+            pltpu.VMEM((RADIX // 2, 2 * points, 2 * LANES), jnp.bfloat16),
+            pltpu.SemaphoreType.DMA((2, halves, RADIX - 1)),
+            pltpu.SemaphoreType.DMA((2, halves, RADIX - 1)),
+            pltpu.SemaphoreType.DMA((2, halves)),
+        ],
+        compiler_params=pltpu.CompilerParams(
+            collective_id=0, has_side_effects=True, vmem_limit_bytes=60 * 1024 * 1024
+        ),
+    )(state, *angle_tables(points))
+
+
 def solution(mesh):
+    devices = mesh.shape["lon"]
+
+    def local(state):
+        points, fields, lat_dev = state.shape
+        fits = (
+            devices == RADIX
+            and fields == RADIX * SUBLANES
+            and points == 2 * LANES
+            and lat_dev == 2 * LANES
+        )
+        return fused_local(state) if fits else dense_local(state)
+
     return jax.shard_map(
         local,
         mesh=mesh,

time: 968 us -> 738 us (0.76)
  Pallas kernels: 0 us -> 726 us
  blocking collectives: 366 us -> 0 us
  waiting for transfers between devices: 298 us -> 0 us
  matrix products: 130 us -> 0 us
  local copies, waits for them, and re-layouts: 93 us -> 11.8 us
  other arithmetic: 69.9 us -> 0 us
    pallas_call x0 -> x1, Pallas kernels: none -> 726 us  [fused_local(): pl.pallas_call(functools.partial(kernel, halves), out_shape=jax.ShapeDtyp...]
    all_to_all x1 -> x0, blocking collectives: 366 us -> none  [local(): lax.all_to_all(spectrum, 'lon', split_axis=1, concat_axis=2, tiled=True)]
    all_to_all x1 -> x0, waiting for transfers between devices: 298 us -> none  [local(): lax.all_to_all(columns, 'lon', split_axis=1, concat_axis=0, tiled=True)]
    dot_general x2 -> x0, matrix products: 130 us -> none  [the longest x1 68.6 us: dense_spectrum(): jnp.dot(jnp.cos(angles) * factor, gathered, precision=lax.Precision.HIGHE...]
    dot_general x2 -> x0, other arithmetic: 63.4 us -> none  [the longest x1 31.9 us: dense_spectrum(): jnp.dot(-jnp.sin(angles) * factor, gathered, precision=lax.Precision.HIGH...]
    all_to_all x2 -> x0, local copies, waits for them, and re-layouts: 36.1 us -> none  [the longest x1 19.8 us: local(): lax.all_to_all(spectrum, 'lon', split_axis=1, concat_axis=2, tiled=True)]
    another operation x1 -> x0, local copies, waits for them, and re-layouts: 21.3 us -> none  [dense_spectrum(): return jnp.stack([real_part, imag_part])]
    reshape x1 -> x0, local copies, waits for them, and re-layouts: 18 us -> none  [local(): return shares.reshape(2, shares.shape[1], fields, lat_dev)]
  transfers between devices with their start and end apart: 1 -> 0, of which waited for: 1 -> 0; matrix products, arithmetic and copies ran while one was open for 7% -> 0% of each run, Pallas kernels for 0% -> 0%
where the time goes in v1:
time: 738 us
  Pallas kernels  726 us (98%)
  local copies, waits for them, and re-layouts  11.8 us (2%)
    pallas_call x1, Pallas kernels, fused_local(): pl.pallas_call(functools.partial(kernel, halves), out_shape=jax.ShapeDtyp...  726 us

profile of v1, /device:TPU:13, one launch (start us, length us, event | category | flops | bytes accessed | tf_op | source)
XLA Modules:
  0.0 737.6 jit_solution(16374336549797410916)
XLA Ops:
  0.0 725.8 %shard_map.55 = f32[2,128,64,256]{3,2,1,0:T(8,128)} custom-call(f32[256,64,256]{2,1,0:T(8,128)} %state.1, f32[128,256]{1,0:T(8,128)} %constant.8.clone.cos_base, f32[128,256]{1,0:T(8,128)} %constant.9.clone.sin_base, f32[8,256]{1,0:T(8,128)} %constant.10.clone.cos_turn, f32[8,256]{1,0:T(8,128)} %constant.11.clone.sin_turn), custom_call_target="tpu_custom_call" | custom-call | tf_op jit(solution)/shard_map/pallas_call | solution.py:270
  725.8 11.8 %copy.7 = f32[2,128,64,256]{3,2,1,0:T(8,128)} copy(f32[2,128,64,256]{3,2,1,0:T(8,128)} %shard_map.55) | data formatting | bytes 33554432

commit v2 on v1

--- a/solution.py
+++ b/solution.py
@@ -269,7 +269,7 @@
     half_shape = (2, modes, SUBLANES, LANES)
     return pl.pallas_call(
         functools.partial(kernel, halves),
-        out_shape=jax.ShapeDtypeStruct((2, modes, fields, lat_dev), jnp.float32),
+        out_shape=pltpu.VMEM((2, modes, fields, lat_dev), jnp.float32),
         in_specs=[hbm] + [vmem] * 4,
         out_specs=hbm,
         scratch_shapes=[
@@ -284,7 +284,7 @@
             pltpu.SemaphoreType.DMA((2, halves)),
         ],
         compiler_params=pltpu.CompilerParams(
-            collective_id=0, has_side_effects=True, vmem_limit_bytes=60 * 1024 * 1024
+            collective_id=0, has_side_effects=True, vmem_limit_bytes=41 * 1024 * 1024
         ),
     )(state, *angle_tables(points))
 

time: 738 us -> 732 us (level)
  no operation moved by 1% of the time
where the time goes in v2:
time: 732 us
  Pallas kernels  726 us (99%)
    pallas_call x1, Pallas kernels, fused_local(): pl.pallas_call(functools.partial(kernel, halves), out_shape=pltpu.VMEM((2...  726 us

profile of v2, /device:TPU:13, one launch (start us, length us, event | category | flops | bytes accessed | tf_op | source)
XLA Modules:
  0.0 731.8 jit_solution(13366672594763235732)
XLA Ops:
  0.0 725.7 %shard_map.55 = f32[2,128,64,256]{3,2,1,0:T(8,128)S(1)} custom-call(f32[256,64,256]{2,1,0:T(8,128)} %state.1, f32[128,256]{1,0:T(8,128)} %constant.8.clone.cos_base, f32[128,256]{1,0:T(8,128)} %constant.9.clone.sin_base, f32[8,256]{1,0:T(8,128)} %constant.10.clone.cos_turn, f32[8,256]{1,0:T(8,128)} %constant.11.clone.sin_turn), custom_call_target="tpu_custom_call" | custom-call | tf_op jit(solution)/shard_map/pallas_call | solution.py:270
  725.7 6.2 copy.7
